TPU v7x, 32 devices: a whole 2x2x4 slice. The times are simulated.
32 devices in a mesh: dp: 4 (over z), stage: 2 (over y), tp: 4 (over x, core).
Axes of the slice: x: 2, y: 2, z: 4, core: 2. Of those that a mesh axis runs over, the one named last changes fastest.
Arguments:
- act_mb1: bfloat16 [2, 16, 14, 14, 512], P('stage', ('dp', 'tp'))
- act_mb2: bfloat16 [2, 16, 14, 14, 512], P('stage', ('dp', 'tp'))
- conv_w: bfloat16 [2, 3, 3, 512, 512], P('stage', None, None, 'tp')
- gamma_scale: float32 [2, 512], P('stage', 'tp')
- beta_shift: float32 [2, 512], P('stage', 'tp')
- dz_mb1: bfloat16 [2, 16, 14, 14, 512], P('stage', 'dp', None, None, 'tp')
- dz_mb2: bfloat16 [2, 16, 14, 14, 512], P('stage', 'dp', None, None, 'tp')
Outputs:
- output 1: bfloat16 [2, 16, 14, 14, 512], P('stage', 'dp', None, None, 'tp')
- output 2: bfloat16 [2, 16, 14, 14, 512], P('stage', 'dp', None, None, 'tp')
- output 3: bfloat16 [2, 16, 14, 14, 512], P('stage', ('dp', 'tp'))
- output 4: bfloat16 [2, 16, 14, 14, 512], P('stage', ('dp', 'tp'))
- output 5: float32 [2, 3, 3, 512, 512], P('stage', None, None, 'tp')
All inputs are finite; a program needn't handle non-finite values.
Results may differ from a plain program's by a relative error of at most 0.00363.
Values are sent between devices in bfloat16 or wider.
A program may use at most 1 GiB of HBM per device.

v0:
```python
import jax
import jax.numpy as jnp
from jax import lax
from jax.sharding import PartitionSpec as P


def conv_forward(act_in, kernel):
    return lax.conv_general_dilated(act_in, kernel, (1, 1), 'SAME', dimension_numbers=('NHWC', 'HWIO', 'NHWC'), preferred_element_type=jnp.float32)


def conv_input_grad(grad_out, kernel):
    return lax.conv_general_dilated(grad_out, lax.rev(kernel, (0, 1)), (1, 1), 'SAME', dimension_numbers=('NHWC', 'HWOI', 'NHWC'), preferred_element_type=jnp.float32)


def conv_kernel_grad(act_in, grad_out):
    return lax.conv_general_dilated(act_in, grad_out, (1, 1), ((1, 1), (1, 1)), dimension_numbers=('CHWN', 'IHWO', 'HWNC'), preferred_element_type=jnp.float32)


def solution(mesh):
    act_spec = P('stage', ('dp', 'tp'), None, None, None)
    w_spec = P('stage', None, None, 'tp', None)
    vec_spec = P('stage', 'tp')
    dz_spec = P('stage', 'dp', None, None, 'tp')

    def device_body(act_mb1, act_mb2, conv_w, gamma_scale, beta_shift, dz_mb1, dz_mb2):
        stage_idx = lax.axis_index('stage')
        kernel = conv_w[0]
        gain_vec = gamma_scale[0]
        shift_vec = beta_shift[0]

        def forward(act_in):
            act_swap = lax.all_to_all(act_in, 'tp', 3, 0, tiled=True)
            act_moved = lax.ppermute(act_swap, 'stage', [(0, 1)])
            part_sum = conv_forward(act_moved, kernel)
            pre_act = lax.psum_scatter(part_sum, 'tp', scatter_dimension=3, tiled=True)
            y_lin = pre_act * gain_vec + shift_vec
            z_out = jnp.maximum(y_lin, 0.0).astype(jnp.bfloat16)
            return act_moved, y_lin, z_out

        def backward(act_moved, y_lin, dz_in):
            g_local = jnp.where(y_lin > 0, dz_in * gain_vec, 0.0).astype(jnp.bfloat16)
            g_full = lax.all_gather(g_local, 'tp', axis=3, tiled=True)
            dact_local = conv_input_grad(g_full, kernel).astype(jnp.bfloat16)
            d_kernel = conv_kernel_grad(act_moved, g_full)
            dact_back = lax.ppermute(dact_local, 'stage', [(1, 0)])
            dact_out = lax.all_to_all(dact_back, 'tp', 0, 3, tiled=True)
            return dact_out, d_kernel

        moved_one, y_one, z_one = forward(act_mb1[0])
        moved_two, y_two, z_two = forward(act_mb2[0])
        dact_one, dw_one = backward(moved_one, y_one, dz_mb1[0])
        dact_two, dw_two = backward(moved_two, y_two, dz_mb2[0])
        dw_total = lax.psum(dw_one + dw_two, 'dp')
        on_first = stage_idx == 0
        on_second = stage_idx == 1
        return (jnp.where(on_second, z_one, 0)[None], jnp.where(on_second, z_two, 0)[None], jnp.where(on_first, dact_one, 0)[None], jnp.where(on_first, dact_two, 0)[None], jnp.where(on_second, dw_total, 0.0)[None])

    return jax.shard_map(device_body, mesh=mesh, in_specs=(act_spec, act_spec, w_spec, vec_spec, vec_spec, dz_spec, dz_spec), out_specs=(dz_spec, dz_spec, act_spec, act_spec, w_spec), check_vma=False)
```

profile of v0, /device:TPU:4, one launch (start us, length us, event | category | flops | bytes accessed | tf_op | source)
XLA Modules:
  0.0 381.9 jit_solution(15645090287766417960)
XLA Ops:
  7.2 3.8 %copy.36 = bf16[1,1,14,14,512]{3,2,4,1,0:T(8,128)(2,1)} copy(bf16[1,1,14,14,512]{4,3,2,1,0:T(8,128)(2,1)} %param.7) | data formatting | bytes 401408 | tf_op args[0]
  13.0 2.4 reshape.100
  15.4 8.3 %all_to_all.54 = bf16[4,2,12544]{2,1,0:T(2,128)(2,1)} all-to-all(bf16[4,2,12544]{2,1,0:T(2,128)(2,1)S(1)} %reshape.100), channel_id=1, replica_groups=mesh['dp'=4,'stage'=2,'tp'=4] {'tp'}, dimensions={0} | all-to-all | bytes 401408 | tf_op jit(solution)/shard_map/all_to_all | solution.py:32
  23.7 3.1 reshape.101
  30.3 7.3 %collective-permute-done = bf16[4,14,14,128]{3,0,2,1:T(4,128)(2,1)S(1)} collective-permute-done((bf16[4,14,14,128]{3,0,2,1:T(4,128)(2,1)S(1)}, bf16[4,14,14,128]{3,0,2,1:T(4,128)(2,1)S(1)}, u32[]{:S(2)}, u32[]{:S(2)}) %collective-permute-start) | collective-permute-done | bytes 200736 | tf_op jit(solution)/shard_map/ppermute | solution.py:33
  41.2 2.5 reshape.60
  45.3 29.0 %copy.58 = f32[4,14,14,512]{0,2,1,3:T(8,128)} copy(f32[4,14,14,512]{3,2,0,1:T(8,128)S(1)} %slice_bitcast_fusion.1) | data formatting | bytes 3211264
  74.3 32.4 %reshape.96 = f32[512,784]{1,0:T(8,128)} reshape(f32[512,14,14,4]{3,2,1,0:T(8,128)} %bitcast.105) | data formatting | bytes 3211264
  107.7 2.9 copy.42
  112.5 2.4 reshape.102
  114.9 8.3 %all_to_all.55 = bf16[4,2,12544]{2,1,0:T(2,128)(2,1)} all-to-all(bf16[4,2,12544]{2,1,0:T(2,128)(2,1)S(1)} %reshape.102), channel_id=1, replica_groups=mesh['dp'=4,'stage'=2,'tp'=4] {'tp'}, dimensions={0} | all-to-all | bytes 401408 | tf_op jit(solution)/shard_map/all_to_all | solution.py:32
  123.2 3.1 reshape.103
  129.7 7.3 %collective-permute-done.1 = bf16[4,14,14,128]{3,0,2,1:T(4,128)(2,1)S(1)} collective-permute-done((bf16[4,14,14,128]{3,0,2,1:T(4,128)(2,1)S(1)}, bf16[4,14,14,128]{3,0,2,1:T(4,128)(2,1)S(1)}, u32[]{:S(2)}, u32[]{:S(2)}) %collective-permute-start.1) | collective-permute-done | bytes 200736 | tf_op jit(solution)/shard_map/ppermute | solution.py:33
  140.1 2.5 reshape.67
  144.2 29.0 %copy.60 = f32[4,14,14,512]{0,2,1,3:T(8,128)} copy(f32[4,14,14,512]{3,2,0,1:T(8,128)S(1)} %slice_bitcast_fusion) | data formatting | bytes 3211264
  173.2 32.4 %reshape.98 = f32[512,784]{1,0:T(8,128)} reshape(f32[512,14,14,4]{3,2,1,0:T(8,128)} %bitcast.106) | data formatting | bytes 3211264
  206.0 8.6 %reshape.97 = f32[128,14,14,4]{3,2,1,0:T(8,128)} reshape(f32[128,784]{1,0:T(8,128)} %reduce-scatter.7.cloned.1.call-done) | data formatting | bytes 802816
  214.6 9.2 %copy.59 = f32[4,14,14,128]{3,0,2,1:T(4,128)S(1)} copy(f32[4,14,14,128]{0,2,1,3:T(8,128)} %bitcast.107) | data formatting | bytes 802816
  223.8 11.8 %reduce-scatter.9.cloned.1.call-done = f32[128,784]{1,0:T(8,128)} async-done(((f32[512,784]{1,0:T(8,128)}), f32[128,784]{1,0:T(8,128)}) %reduce-scatter.9.cloned.1.call-update) | async-done | bytes 401424
  235.6 8.6 %reshape.99 = f32[128,14,14,4]{3,2,1,0:T(8,128)} reshape(f32[128,784]{1,0:T(8,128)} %reduce-scatter.9.cloned.1.call-done) | data formatting | bytes 802816
  244.2 9.2 %copy.61 = f32[4,14,14,128]{3,0,2,1:T(4,128)S(1)} copy(f32[4,14,14,128]{0,2,1,3:T(8,128)} %bitcast.108) | data formatting | bytes 802816
  253.8 8.2 %all_gather.7 = bf16[4,14,14,512]{3,0,2,1:T(4,128)(2,1)S(1)} all-gather(bf16[4,14,14,128]{3,0,2,1:T(4,128)(2,1)S(1)} %get-tuple-element.5), channel_id=1, replica_groups=mesh['dp'=4,'stage'=2,'tp'=4] {'tp'}, dimensions={3}, use_global_device_ids=true | all-gather | bytes 1003520 | tf_op jit(solution)/shard_map/all_gather | solution.py:42
  262.1 9.0 %all_gather.6 = bf16[4,14,14,512]{3,0,2,1:T(4,128)(2,1)S(1)} all-gather(bf16[4,14,14,128]{3,0,2,1:T(4,128)(2,1)S(1)} %get-tuple-element.6), channel_id=1, replica_groups=mesh['dp'=4,'stage'=2,'tp'=4] {'tp'}, dimensions={3}, use_global_device_ids=true | all-gather | bytes 1003520 | tf_op jit(solution)/shard_map/all_gather | solution.py:42
  273.4 3.6 convolution_add_fusion
  281.7 2.7 collective-permute-start.3
  285.5 2.3 fusion.35
  290.3 3.4 all-to-all-start.3
  295.4 3.7 all-to-all-done.3
  299.1 3.4 all-to-all-start.2
  303.4 4.5 %all-to-all-done.2 = bf16[4,14,14,128]{3,2,1,0:T(8,128)(2,1)S(1)} async-done(((bf16[4,14,14,128]{3,2,1,0:T(8,128)(2,1)}), bf16[4,14,14,128]{3,2,1,0:T(8,128)(2,1)S(1)}, u32[]{:S(2)}, u32[]{:S(2)}) %all-to-all-start.2) | async-done | bytes 200736 | tf_op jit(solution)/shard_map/all_to_all | solution.py:46
  308.8 63.3 %all-reduce.2.cloned.1.call-done = f32[3,3,128,512]{3,2,1,0:T(8,128)} async-done(((f32[3,3,128,512]{3,2,1,0:T(8,128)}), f32[3,3,128,512]{3,2,1,0:T(8,128)}) %all-reduce.2.cloned.1.call-update) | async-done | bytes 2359312 | tf_op jit(solution)/shard_map/psum | solution.py:53
  372.0 3.4 select_bitcast_fusion
  (68 shorter events, 36.1 us)
Async XLA Ops:
  7.2 31.2 %copy-start = (bf16[1,3,3,128,512]{4,3,2,1,0:T(8,128)(2,1)S(1)}, bf16[1,3,3,128,512]{4,3,2,1,0:T(8,128)(2,1)}, u32[]{:S(2)}) copy-start(bf16[1,3,3,128,512]{4,3,2,1,0:T(8,128)(2,1)} %param.9) | copy-start | bytes 3538948
  7.2 198.8 %reduce-scatter.7.cloned.1.call-start = ((), (), s32[]{:S(2)}) async-start(), calls=%async_computation.7 | async-start | bytes 2293760
  26.8 11.5 %copy-start.9 = (pred[32,2]{0,1:T(4,128)(4,1)S(1)}, pred[32,2]{0,1:T(4,128)(4,1)}, u32[]{:S(2)}) copy-start(pred[32,2]{0,1:T(4,128)(4,1)} %constant.38) | copy-start | bytes 196
  29.0 8.6 %collective-permute-start = (bf16[4,14,14,128]{3,0,2,1:T(4,128)(2,1)S(1)}, bf16[4,14,14,128]{3,0,2,1:T(4,128)(2,1)S(1)}, u32[]{:S(2)}, u32[]{:S(2)}) collective-permute-start(bf16[4,14,14,128]{3,0,2,1:T(4,128)(2,1)S(1)} %bitcast.119), channel_id=1, source_target_pairs={{0,4},{1,5},{2,6},{3,7},{8,12},{9,13},{10,14},{11,15},{16,20},{17,... | collective-permute-start | bytes 602120 | tf_op jit(solution)/shard_map/ppermute | solution.py:33
  37.6 0.7 copy-start.3
  106.7 0.9 copy-start.2
  106.8 128.8 %reduce-scatter.9.cloned.1.call-start = ((), (), s32[]{:S(2)}) async-start(), calls=%async_computation.8 | async-start | bytes 2293760
  128.4 8.6 %collective-permute-start.1 = (bf16[4,14,14,128]{3,0,2,1:T(4,128)(2,1)S(1)}, bf16[4,14,14,128]{3,0,2,1:T(4,128)(2,1)S(1)}, u32[]{:S(2)}, u32[]{:S(2)}) collective-permute-start(bf16[4,14,14,128]{3,0,2,1:T(4,128)(2,1)S(1)} %bitcast.120), channel_id=1, source_target_pairs={{0,4},{1,5},{2,6},{3,7},{8,12},{9,13},{10,14},{11,15},{16,20},{17,... | collective-permute-start | bytes 602120 | tf_op jit(solution)/shard_map/ppermute | solution.py:33
  205.7 166.4 %all-reduce.2.cloned.1.call-start = ((), (), s32[]{:S(2)}) async-start(), calls=%async_computation.6 | async-start | bytes 4718592 | tf_op jit(solution)/shard_map/psum | solution.py:53
  244.2 9.2 %copy-start.5 = (bf16[1,4,14,14,128]{4,1,3,2,0:T(4,128)(2,1)S(1)}, bf16[1,4,14,14,128]{4,1,3,2,0:T(4,128)(2,1)}, u32[]{:S(2)}) copy-start(bf16[1,4,14,14,128]{4,1,3,2,0:T(4,128)(2,1)} %param.13) | copy-start | bytes 602116
  244.2 9.3 %copy-start.6 = (bf16[1,4,14,14,128]{4,1,3,2,0:T(4,128)(2,1)S(1)}, bf16[1,4,14,14,128]{4,1,3,2,0:T(4,128)(2,1)}, u32[]{:S(2)}) copy-start(bf16[1,4,14,14,128]{4,1,3,2,0:T(4,128)(2,1)} %param.12) | copy-start | bytes 602116
  244.2 9.3 %copy-start.7 = (f32[1,128]{1,0:T(1,128)S(1)}, f32[1,128]{1,0:T(1,128)}, u32[]{:S(2)}) copy-start(f32[1,128]{1,0:T(1,128)} %param.11) | copy-start | bytes 1540
  244.2 9.3 %copy-start.8 = (f32[1,128]{1,0:T(1,128)S(1)}, f32[1,128]{1,0:T(1,128)}, u32[]{:S(2)}) copy-start(f32[1,128]{1,0:T(1,128)} %param.10) | copy-start | bytes 1540
  262.1 9.0 %copy-start.1 = (bf16[4,14,14,512]{3,0,2,1:T(4,128)(2,1)}, bf16[4,14,14,512]{3,0,2,1:T(4,128)(2,1)S(1)}, u32[]{:S(2)}) copy-start(bf16[4,14,14,512]{3,0,2,1:T(4,128)(2,1)S(1)} %all_gather.7) | copy-start | bytes 2408452
  271.1 2.3 copy-start.4
  281.7 7.8 %collective-permute-start.3 = (bf16[4,14,14,128]{3,2,0,1:T(8,128)(2,1)S(1)}, bf16[4,14,14,128]{3,2,0,1:T(8,128)(2,1)S(1)}, u32[]{:S(2)}, u32[]{:S(2)}) collective-permute-start(bf16[4,14,14,128]{3,2,0,1:T(8,128)(2,1)S(1)} %slice_bitcast_fusion.2), channel_id=1, source_target_pairs={{4,0},{5,1},{6,2},{7,3},{12,8},{13,9},{14,10},{15,11},{20,16},{21,... | collective-permute-start | bytes 602120 | tf_op jit(solution)/shard_map/ppermute | solution.py:45
  288.0 6.7 %collective-permute-start.2 = (bf16[4,14,14,128]{3,2,0,1:T(8,128)(2,1)S(1)}, bf16[4,14,14,128]{3,2,0,1:T(8,128)(2,1)S(1)}, u32[]{:S(2)}, u32[]{:S(2)}) collective-permute-start(bf16[4,14,14,128]{3,2,0,1:T(8,128)(2,1)S(1)} %slice_bitcast_fusion.3), channel_id=1, source_target_pairs={{4,0},{5,1},{6,2},{7,3},{12,8},{13,9},{14,10},{15,11},{20,16},{21,... | collective-permute-start | bytes 602120 | tf_op jit(solution)/shard_map/ppermute | solution.py:45
  290.3 8.8 %all-to-all-start.3 = ((bf16[4,14,14,128]{3,2,1,0:T(8,128)(2,1)}), bf16[4,14,14,128]{3,2,1,0:T(8,128)(2,1)S(1)}, u32[]{:S(2)}, u32[]{:S(2)}) async-start(bf16[4,14,14,128]{3,2,1,0:T(8,128)(2,1)} %copy.56), calls=%async_computation.3 | async-start | bytes 458752 | tf_op jit(solution)/shard_map/all_to_all | solution.py:46
  299.1 8.8 %all-to-all-start.2 = ((bf16[4,14,14,128]{3,2,1,0:T(8,128)(2,1)}), bf16[4,14,14,128]{3,2,1,0:T(8,128)(2,1)S(1)}, u32[]{:S(2)}, u32[]{:S(2)}) async-start(bf16[4,14,14,128]{3,2,1,0:T(8,128)(2,1)} %copy.51), calls=%async_computation.2 | async-start | bytes 458752 | tf_op jit(solution)/shard_map/all_to_all | solution.py:46
Sparse Core Ops, SparseCore 0:
  106.9 29.7 reduce-scatter.6
  205.8 29.7 reduce-scatter.8
  277.2 94.8 all-reduce.1
where the time goes:
time: 384 us; the launch traced here: 382 us
  local copies, waits for them, and re-layouts  204 us (53%)
  waiting for transfers between devices  98.3 us (26%)
  blocking collectives  33.8 us (9%)
  between operations  14.2 us (4%)
  starting transfers between devices  13.9 us (4%)
  matrix products  13.2 us (3%)
  other arithmetic  5 us (1%)
    unnamed x36, local copies, waits for them, and re-layouts  181 us
    psum x1, waiting for transfers between devices, device_body(): dw_total = lax.psum(dw_one + dw_two, 'dp')  63.3 us
    all_gather x2, blocking collectives, backward(): g_full = lax.all_gather(g_local, 'tp', axis=3, tiled=True)  17.2 us
    all_to_all x2, blocking collectives, forward(): act_swap = lax.all_to_all(act_in, 'tp', 3, 0, tiled=True)  16.6 us
    ppermute x2, waiting for transfers between devices, forward(): act_moved = lax.ppermute(act_swap, 'stage', [(0, 1)])  14.7 us
    unnamed x5, waiting for transfers between devices  11.9 us
    conv_general_dilated x10, local copies, waits for them, and re-layouts, conv_forward(): lax.conv_general_dilated(act_in, kernel, (1, 1), 'SAME', dimension_number...  11.3 us
    all_to_all x2, waiting for transfers between devices, backward(): dact_out = lax.all_to_all(dact_back, 'tp', 0, 3, tiled=True)  8.2 us
  transfers between devices with their start and end apart: 9, of which 7 were waited for; matrix products, arithmetic and copies ran while one was open for 29% of the time, Pallas kernels for 0%

commit v1 on v0

v1 whole, which is shorter than its diff:
```python
import functools

import jax
import jax.numpy as jnp
from jax import lax
from jax.experimental import pallas as pl
from jax.experimental.pallas import tpu as pltpu
from jax.sharding import PartitionSpec as P

MESH = pl.DeviceIdType.MESH
BF = jnp.bfloat16
F32 = jnp.float32

SIDE = 14
LW = 16
NI = 4
IL = 15
ML = NI * IL
PL = 66
TL = 64
MR = ML * LW
DENSE = NI * SIDE * SIDE


def row_target(idx):
    h = (idx * 1171) >> 16
    rem = idx - h * 56
    w = rem >> 2
    n = rem & 3
    return n * (IL * LW) + h * LW + w


def kernel(act1, act2, conv_w, gamma, beta, dz1, dz2,
           z1, z2, da1, da2, dw,
           kbuf, kown, arx, aoth, apad, dzv, dpad, zpad, pmat, grx, gpad, at3, dsend,
           ksend, krecv, kloc, lsem, asend, arecv, afwd, osend, orecv,
           gzs, gxs, gss, gfs, grecv, dsem, drecv):
    dp = lax.axis_index("dp")
    st = lax.axis_index("stage")
    tp = lax.axis_index("tp")
    sib = tp + 1 - 2 * (tp % 2)
    xnb = (tp + 2) % 4
    xsib = (sib + 2) % 4
    acts = (act1, act2)
    dzs = (dz1, dz2)
    zs = (z1, z2)
    das = (da1, da2)

    def remote(src, dst, ss, rs, dev):
        return pltpu.make_async_remote_copy(src_ref=src, dst_ref=dst, send_sem=ss, recv_sem=rs,
                                            device_id=dev, device_id_type=MESH)

    def lane(i):
        return pl.ds(pl.multiple_of(i * 128, 128), 128)

    def own_a(mb, slot, dev):
        return remote(acts[mb].at[0, 0], arx.at[mb, tp], asend.at[mb, slot], arecv.at[mb, tp], dev)

    def oth_a(mb, j, c):
        return remote(acts[mb].at[0, 0, :, :, pl.ds(c * 128, 128)], aoth.at[mb, dp, tp],
                      osend.at[mb, j, c], orecv.at[mb, dp, tp], ((dp + j) % 4, 1, c))

    barrier = pltpu.get_barrier_semaphore()

    @pl.when(st == 0)
    def _():
        def hello(i, _):
            pl.semaphore_signal(barrier, inc=1, device_id=(i // 4, 1, i % 4), device_id_type=MESH)
            return 0
        lax.fori_loop(0, 16, hello, 0)
        pl.semaphore_wait(barrier, 16)
        for mb in range(2):
            own_a(mb, 0, (dp, 1, tp)).start()
            own_a(mb, 1, (dp, 1, xnb)).start()
        for mb in range(2):
            zs[mb][...] = jnp.zeros(z1.shape, BF)
        dw[...] = jnp.zeros(dw.shape, F32)
        for mb in range(2):
            own_a(mb, 0, (dp, 1, tp)).wait_send()
            own_a(mb, 1, (dp, 1, xnb)).wait_send()
        for mb in range(2):
            for j in range(1, 4):
                for c in range(4):
                    oth_a(mb, j, c).start()
        for mb in range(2):
            for j in range(1, 4):
                for c in range(4):
                    oth_a(mb, j, c).wait_send()
        for mb in range(2):
            for c in range(4):
                remote(dsend.at[mb, 0], das[mb].at[:, :, pl.ds(c * 128, 128)], dsem.at[mb, c],
                       drecv.at[mb, c], (dp, 1, c)).wait_recv()

    @pl.when(st == 1)
    def _():
        def hello(i, _):
            pl.semaphore_signal(barrier, inc=1, device_id=(i // 4, 0, i % 4), device_id_type=MESH)
            return 0
        lax.fori_loop(0, 16, hello, 0)
        for j in range(1, 4):
            pl.semaphore_signal(barrier, inc=1, device_id=((dp + j) % 4, 1, tp), device_id_type=MESH)
            pl.semaphore_signal(barrier, inc=1, device_id=(dp, 1, (tp + j) % 4), device_id_type=MESH)
        pl.semaphore_wait(barrier, 22)

        def k_copy(j, kw):
            c = (tp + j) % 4
            return remote(conv_w.at[0, :, kw, :, lane(c)],
                          kbuf.at[:, lane(tp), pl.ds(kw * 128, 128)],
                          ksend.at[c, kw], krecv.at[tp, kw], (dp, 1, c))

        def k_wait(j, kw):
            c = (tp + j) % 4
            return remote(conv_w.at[0, :, kw, :, lane(c)],
                          kbuf.at[:, lane(c), pl.ds(kw * 128, 128)],
                          ksend.at[c, kw], krecv.at[c, kw], (dp, 1, c))

        def k_local(kw):
            return pltpu.make_async_copy(conv_w.at[0, :, kw, :, lane(tp)],
                                         kbuf.at[:, lane(tp), pl.ds(kw * 128, 128)], kloc.at[kw])

        for j in (2, 3, 1):
            for kw in range(3):
                k_copy(j, kw).start()
        for kw in range(3):
            k_local(kw).start()
        own_k = pltpu.make_async_copy(conv_w.at[0], kown, lsem.at[0])
        own_k.start()
        for mb in range(2):
            pltpu.make_async_copy(dzs[mb], dzv.at[mb], lsem.at[1 + mb]).start()

        for mb in range(2):
            das[mb][...] = jnp.zeros(da1.shape, BF)
        dw[...] = jnp.zeros(dw.shape, F32)
        apad[...] = jnp.zeros(apad.shape, BF)
        gpad[...] = jnp.zeros(gpad.shape, BF)

        def place(rows, cols, fixed):
            a = lax.broadcasted_iota(jnp.int32, (rows, cols), 0)
            b = lax.broadcasted_iota(jnp.int32, (rows, cols), 1)
            hit = (row_target(b) == a) if fixed else (row_target(a) == b)
            return jnp.where(hit, 1.0, 0.0).astype(BF)

        for r in range(4):
            rows = MR // 4
            a = lax.broadcasted_iota(jnp.int32, (rows, DENSE), 0) + r * rows
            b = row_target(lax.broadcasted_iota(jnp.int32, (1, DENSE), 1))
            pmat[r * rows:(r + 1) * rows, :DENSE] = jnp.where(a == b, 1.0, 0.0).astype(BF)
        for mb in range(2):
            pltpu.make_async_copy(dzs[mb], dzv.at[mb], lsem.at[1 + mb]).wait()
            for r in range(4):
                rows = MR // 4
                dpad[mb, r * rows:(r + 1) * rows, :] = jnp.dot(
                    pmat[r * rows:(r + 1) * rows, :DENSE], dzv[mb],
                    preferred_element_type=F32).astype(BF)
        for r in range(7):
            rows = DENSE // 7
            a = row_target(lax.broadcasted_iota(jnp.int32, (rows, 1), 0) + r * rows)
            b = lax.broadcasted_iota(jnp.int32, (rows, MR), 1)
            pmat[r * rows:(r + 1) * rows, :MR] = jnp.where(a == b, 1.0, 0.0).astype(BF)
        own_k.wait()

        def g_slot(mb, d, t):
            return grx.at[mb, d, t]

        def g_z(mb, j):
            return remote(g_slot(mb, dp, tp), g_slot(mb, dp, tp), gzs.at[mb, j], grecv.at[mb, dp, tp],
                          ((dp + j) % 4, 1, tp))

        def g_x(mb, d):
            return remote(g_slot(mb, d, tp), g_slot(mb, d, tp), gxs.at[mb, d], grecv.at[mb, d, tp],
                          (dp, 1, xnb))

        def g_s(mb, d):
            return remote(g_slot(mb, d, tp), g_slot(mb, d, tp), gss.at[mb, d], grecv.at[mb, d, tp],
                          (dp, 1, sib))

        def g_f(mb, d):
            return remote(g_slot(mb, d, xnb), g_slot(mb, d, xnb), gfs.at[mb, d], grecv.at[mb, d, xnb],
                          (dp, 1, sib))

        def g_wait(mb, d, t):
            remote(g_slot(mb, d, t), g_slot(mb, d, t), gss.at[mb, d], grecv.at[mb, d, t],
                   (dp, 1, sib)).wait_recv()

        def a_fwd(mb, t):
            return remote(arx.at[mb, t], arx.at[mb, t], afwd.at[mb, t], arecv.at[mb, t], (dp, 1, sib))

        def a_wait(mb, t):
            remote(arx.at[mb, t], arx.at[mb, t], afwd.at[mb, t], arecv.at[mb, t],
                   (dp, 1, sib)).wait_recv()

        def spread_g(mb, d):
            def line(i, _):
                n = i // SIDE
                l = 1 + n * IL + (i - n * SIDE)
                for t in range(4):
                    gpad[l, 0:SIDE, t * 128:(t + 1) * 128] = grx[mb, d, t, i]
                return 0
            lax.fori_loop(0, NI * SIDE, line, 0)

        def d_out(mb, i):
            return remote(dsend.at[mb, i], das0.at[mb] if False else (da1, da2)[0], dsem.at[mb, i],
                          drecv.at[mb, tp], (dp, 0, i))

        for mb in range(2):
            a_wait(mb, tp)
            a_fwd(mb, tp).start()
            a_wait(mb, xnb)
            a_fwd(mb, xnb).start()
            a_wait(mb, sib)
            a_wait(mb, xsib)
            for n in range(NI):
                def line(h, _):
                    apad[1 + n * IL + h, 0:SIDE, :] = arx[mb, n, h]
                    return 0
                lax.fori_loop(0, SIDE, line, 0)
            if mb == 0:
                for kw in range(3):
                    k_local(kw).wait()
                for j in (2, 3, 1):
                    for kw in range(3):
                        k_wait(j, kw).wait_recv()

            def forward(i, _):
                lhs = jnp.concatenate([apad[pl.ds(30 * i + kh, 30)].reshape(480, 512) for kh in range(3)], axis=1)
                part = jnp.dot(lhs, kbuf[...].reshape(1536, 384), preferred_element_type=F32)
                pre = pltpu.roll(part[:, 0:128], 1, 0) + part[:, 128:256] + pltpu.roll(part[:, 256:384], 479, 0)
                gain = gamma[...]
                y = pre * gain + beta[...]
                rows = pl.ds(pl.multiple_of(480 * i, 480), 480)
                zpad[rows, :] = jnp.maximum(y, 0.0).astype(BF)
                dval = dpad[mb, rows, :].astype(F32)
                g = jnp.where(y > 0, dval * gain, 0.0).astype(BF).reshape(30, LW, 128)
                for k in range(30):
                    n, h = divmod(k, IL)
                    if h < SIDE:
                        grx[mb, dp, tp, (2 * i + n) * SIDE + h] = g[k, 0:SIDE, :]
                return 0
            lax.fori_loop(0, 2, forward, 0)
            g_x(mb, dp).start()
            g_s(mb, dp).start()
            for j in (1, 3, 2):
                g_z(mb, j).start()
            for r in range(7):
                rows = DENSE // 7
                zs[mb][r * rows:(r + 1) * rows, :] = jnp.dot(
                    pmat[r * rows:(r + 1) * rows, :MR], zpad[...], preferred_element_type=F32).astype(BF)
            g_wait(mb, dp, xnb)
            g_f(mb, dp).start()
            if mb == 1:
                for j in (1, 3, 2):
                    d = (dp + j) % 4
                    g_wait(0, d, tp)
                    g_x(0, d).start()
                    g_s(0, d).start()
            g_wait(mb, dp, sib)
            g_wait(mb, dp, xsib)
            spread_g(mb, dp)

            def backward(i, _):
                lhs = jnp.concatenate([gpad[pl.ds(30 * i + 2 - kh, 30)].reshape(480, 512) for kh in range(3)], axis=1)
                rhs = jnp.concatenate([kown[kh].reshape(384, 512) for kh in range(3)], axis=1)
                part = lax.dot_general(lhs, rhs, (((1,), (1,)), ((), ())), preferred_element_type=F32)
                da = pltpu.roll(part[:, 0:128], 479, 0) + part[:, 128:256] + pltpu.roll(part[:, 256:384], 1, 0)
                da = da.astype(BF).reshape(30, LW, 128)
                for k in range(30):
                    n, h = divmod(k, IL)
                    if h < SIDE:
                        dsend[mb, 2 * i + n, h] = da[k, 0:SIDE, :]
                return 0
            lax.fori_loop(0, 2, backward, 0)
            for i in range(NI):
                remote(dsend.at[mb, i], das[mb].at[:, :, lane(tp)], dsem.at[mb, i], drecv.at[mb, tp],
                       (dp, 0, i)).start()

        def chunk(q, _):
            mb = q // 4
            j = q % 4
            d = (dp + j) % 4

            @pl.when(j > 0)
            def _():
                @pl.when(mb == 1)
                def _():
                    g_wait(1, d, tp)
                    g_x(1, d).start()
                    g_s(1, d).start()
                g_wait(mb, d, xnb)
                g_f(mb, d).start()
                g_wait(mb, d, sib)
                g_wait(mb, d, xsib)
                for n in range(NI):
                    remote(aoth.at[mb, d, n], aoth.at[mb, d, n], afwd.at[0, 0], orecv.at[mb, d, n],
                           (dp, 1, sib)).wait_recv()

                def line(i, _):
                    n = i // SIDE
                    apad[1 + n * IL + (i - n * SIDE), 0:SIDE, 0:128] = aoth[mb, d, n, i - n * SIDE]
                    return 0
                lax.fori_loop(0, NI * SIDE, line, 0)

            @pl.when(j == 0)
            def _():
                def line(i, _):
                    n = i // SIDE
                    apad[1 + n * IL + (i - n * SIDE), 0:SIDE, 0:128] = arx[mb, n, i - n * SIDE, :, lane(tp)]
                    return 0
                lax.fori_loop(0, NI * SIDE, line, 0)
            spread_g(mb, d)
            a = apad[1:1 + TL, :, 0:128].reshape(TL * LW, 128).astype(F32)
            at3[0:128, :] = pltpu.roll(a, 1, 0).T.astype(BF)
            at3[128:256, :] = a.T.astype(BF)
            at3[256:384, :] = pltpu.roll(a, TL * LW - 1, 0).T.astype(BF)
            for kh in range(3):
                dw[kh] += jnp.dot(at3[...], gpad[2 - kh:2 - kh + TL].reshape(TL * LW, 512),
                                  preferred_element_type=F32)
            return 0
        lax.fori_loop(0, 8, chunk, 0)

        for j in (2, 3, 1):
            for kw in range(3):
                k_copy(j, kw).wait_send()
        for mb in range(2):
            a_fwd(mb, tp).wait_send()
            a_fwd(mb, xnb).wait_send()
            for j in range(1, 4):
                g_z(mb, j).wait_send()
            for d in range(4):
                g_x(mb, d).wait_send()
                g_s(mb, d).wait_send()
                g_f(mb, d).wait_send()
            for i in range(NI):
                remote(dsend.at[mb, i], das[mb].at[:, :, lane(tp)], dsem.at[mb, i], drecv.at[mb, tp],
                       (dp, 0, i)).wait_send()


def solution(mesh):
    act_spec = P('stage', ('dp', 'tp'), None, None, None)
    w_spec = P('stage', None, None, 'tp', None)
    vec_spec = P('stage', 'tp')
    dz_spec = P('stage', 'dp', None, None, 'tp')
    hbm = pl.BlockSpec(memory_space=pl.ANY)
    vmem = pl.BlockSpec(memory_space=pltpu.VMEM)
    dma = pltpu.SemaphoreType.DMA

    def dense(dz):
        return dz[0].transpose(1, 2, 0, 3).reshape(DENSE, 128)

    def undense(z):
        return z.reshape(SIDE, SIDE, NI, 128).transpose(2, 0, 1, 3)[None]

    def device_body(act_mb1, act_mb2, conv_w, gamma_scale, beta_shift, dz_mb1, dz_mb2):
        z1, z2, da1, da2, dw = pl.pallas_call(
            kernel,
            out_shape=(
                jax.ShapeDtypeStruct((DENSE, 128), BF),
                jax.ShapeDtypeStruct((DENSE, 128), BF),
                jax.ShapeDtypeStruct((SIDE, SIDE, 512), BF),
                jax.ShapeDtypeStruct((SIDE, SIDE, 512), BF),
                jax.ShapeDtypeStruct((3, 384, 512), F32),
            ),
            in_specs=[hbm, hbm, hbm, vmem, vmem, hbm, hbm],
            out_specs=(vmem,) * 5,
            scratch_shapes=[
                pltpu.VMEM((3, 512, 384), BF),
                pltpu.VMEM((3, 3, 128, 512), BF),
                pltpu.VMEM((2, 4, SIDE, SIDE, 512), BF),
                pltpu.VMEM((2, 4, 4, SIDE, SIDE, 128), BF),
                pltpu.VMEM((PL, LW, 512), BF),
                pltpu.VMEM((2, DENSE, 128), BF),
                pltpu.VMEM((2, MR, 128), BF),
                pltpu.VMEM((MR, 128), BF),
                pltpu.VMEM((MR, 1024), BF),
                pltpu.VMEM((2, 4, 4, NI * SIDE, SIDE, 128), BF),
                pltpu.VMEM((PL, LW, 512), BF),
                pltpu.VMEM((384, TL * LW), BF),
                pltpu.VMEM((2, NI, SIDE, SIDE, 128), BF),
                dma((4, 3)), dma((4, 3)), dma((3,)), dma((3,)),
                dma((2, 2)), dma((2, 4)), dma((2, 4)), dma((2, 4, 4)), dma((2, 4, 4)),
                dma((2, 4)), dma((2, 4)), dma((2, 4)), dma((2, 4)), dma((2, 4, 4)),
                dma((2, 4)), dma((2, 4)),
            ],
            compiler_params=pltpu.CompilerParams(
                collective_id=0, has_side_effects=True, vmem_limit_bytes=60 * 1024 * 1024),
        )(act_mb1, act_mb2, conv_w, gamma_scale, beta_shift, dense(dz_mb1), dense(dz_mb2))
        return (undense(z1), undense(z2), da1[None, None], da2[None, None], dw.reshape(1, 3, 3, 128, 512))

    return jax.shard_map(device_body, mesh=mesh, in_specs=(act_spec, act_spec, w_spec, vec_spec, vec_spec, dz_spec, dz_spec), out_specs=(dz_spec, dz_spec, act_spec, act_spec, w_spec), check_vma=False)
```

time: 384 us -> 130 us (0.34)
  the two profiles are of different devices: /device:TPU:4 before, /device:TPU:7 now
where the time goes in v1:
time: 130 us; the launch traced here: 129 us
  Pallas kernels  119 us (92%)
  local copies, waits for them, and re-layouts  9.91 us (8%)
    pallas_call x1, Pallas kernels, device_body(): pl.pallas_call(kernel, out_shape=(jax.ShapeDtypeStruct((DENSE, 128), BF),...  119 us
    unnamed x5, local copies, waits for them, and re-layouts  9.91 us

profile of v1, /device:TPU:7, one launch (start us, length us, event | category | flops | bytes accessed | tf_op | source)
XLA Modules:
  0.0 129.5 jit_solution(4094704063245477653)
XLA Ops:
  0.6 118.9 %shard_map.110 = (bf16[784,128]{1,0:T(8,128)(2,1)}, bf16[784,128]{1,0:T(8,128)(2,1)}, bf16[14,14,512]{2,1,0:T(8,128)(2,1)}, bf16[14,14,512]{2,1,0:T(8,128)(2,1)}, f32[3,384,512]{2,1,0:T(8,128)}) custom-call(bf16[1,1,14,14,512]{4,3,2,1,0:T(8,128)(2,1)} %act1.1, bf16[1,1,14,14,512]{4,3,2,1,0:T(8,128)(2,1)} %act2.1, bf16[1,3,3,128,512]{4,3,2,1,0:T(8,128)(2,1)} %conv_w.1, ...), custom_call_target="tpu_custom_call" | custom-call | tf_op jit(solution)/shard_map/pallas_call | solution.py:353
  119.5 1.7 %copy.17 = bf16[1,4,14,14,128]{4,1,3,2,0:T(4,128)(2,1)} copy(bf16[1,4,14,14,128]{4,1,3,2,0:T(4,128)(2,1)} %bitcast.29) | data formatting | bytes 401408
  121.2 1.7 %copy.18 = bf16[1,4,14,14,128]{4,1,3,2,0:T(4,128)(2,1)} copy(bf16[1,4,14,14,128]{4,1,3,2,0:T(4,128)(2,1)} %bitcast.28) | data formatting | bytes 401408
  122.9 1.6 %copy.19 = bf16[1,1,14,14,512]{4,3,2,1,0:T(8,128)(2,1)} copy(bf16[1,1,14,14,512]{4,3,2,1,0:T(8,128)(2,1)} %bitcast.25) | data formatting | bytes 401408
  124.5 1.6 %copy.20 = bf16[1,1,14,14,512]{4,3,2,1,0:T(8,128)(2,1)} copy(bf16[1,1,14,14,512]{4,3,2,1,0:T(8,128)(2,1)} %bitcast.24) | data formatting | bytes 401408
  126.2 3.3 %copy.21 = f32[1,3,3,128,512]{4,3,2,1,0:T(8,128)} copy(f32[1,3,3,128,512]{4,3,2,1,0:T(8,128)} %bitcast.23) | data formatting | bytes 4718592
